TPU v7x, 32 devices: a whole 2x2x4 slice. The times are simulated.
32 devices in a mesh: member: 2 (over core), tile: 16 (over z, y, x).
Axes of the slice: x: 2, y: 2, z: 4, core: 2. Of those that a mesh axis runs over, the one named last changes fastest.
Arguments:
- ensemble: bfloat16 [40, 7, 32, 2048], P('member', None, None, 'tile'), may hold values from -6 to 6
- control: bfloat16 [40, 32, 2048], P('member', None, 'tile'), may hold values from -6 to 6
- vert_loc: bfloat16 [32, 32], replicated, may hold values from -1 to 1
- obs_source: int32 [8192, 1], P('tile'), may hold values from 0 to 15; in each aligned block of 512 rows (0 to 511, 512 to 1023, ...) at most 64 rows name the same one
- obs_column: int32 [8192], P('tile'), may hold values from 0 to 127
- obs_slot: int32 [8192], P('tile'), may hold values from 0 to 5
- obs_frac: float32 [8192], P('tile'), may hold values from 0 to 1
- obs_count: int32 [16], P('tile'), may hold values from 1 to 512, 4096 in all
Outputs:
- obs_increment: float32 [32, 8192], P(None, 'tile')
Inputs may be any that keep to these rules, and one draw needn't show every extreme that they name: `obs_source`: among the 512 observation slots of one owner tile, at most 64 name the same source tile, and some source tile is named exactly 64 times. `obs_count`: the counts sum to 4096 and one of them is 512.
All inputs are finite; a program needn't handle non-finite values. No bound on the sum of `obs_count` on one device may be relied on, other than what follows from the above.
Results may differ from a plain program's by a relative error of at most 0.0003.
Values sent between devices are 32-bit elements; how exact they have to be, the bound alone decides.
A program may use at most 64 MiB of HBM per device.

v0:
```python
import jax
import jax.numpy as jnp
from jax import lax
from jax.sharding import PartitionSpec as P


def bucket(values, where_to, length):
    return jnp.zeros((length,), values.dtype).at[where_to].set(values)


def on_device(ensemble, control, vert_loc, obs_source, obs_column, obs_slot, obs_frac, obs_count):
    tiles = lax.axis_size("tile")
    obs_dev = obs_column.shape[0]
    capacity = max(4, 2 * obs_dev // tiles)
    weighted = jnp.einsum("lj,kjc->klc", vert_loc, control, preferred_element_type=jnp.float32)
    partial_value = jnp.sum(ensemble.astype(jnp.float32) * weighted[:, None], axis=0)
    increment = lax.psum_scatter(partial_value, "member", scatter_dimension=1, tiled=True)
    slots, levels = (increment.shape[0], increment.shape[1])
    source = obs_source[:, 0]
    hits = (source[:, None] == jnp.arange(tiles, dtype=jnp.int32)[None, :]).astype(jnp.int32)
    rank = jnp.sum((jnp.cumsum(hits, axis=0) - 1) * hits, axis=1)
    flat = source * capacity + rank
    col_buf = bucket(obs_column, flat, tiles * capacity).reshape(tiles, capacity)
    frac = obs_frac[None, :]
    steps = jnp.arange(slots, dtype=jnp.int32)[:, None]
    got_cols = lax.all_to_all(col_buf, "tile", split_axis=0, concat_axis=0, tiled=True)
    picks = jnp.take(increment, got_cols.reshape(-1), axis=2).reshape(
        slots, levels, tiles, capacity
    )
    returned = lax.all_to_all(picks, "tile", split_axis=2, concat_axis=2, tiled=True).reshape(
        slots, levels, tiles * capacity
    )
    columns = jnp.take(returned, flat, axis=2)
    wanted = obs_slot[None, :]
    weights = (1.0 - frac) * (steps == wanted).astype(jnp.float32) + frac * (
        steps == wanted + 1
    ).astype(jnp.float32)
    value = jnp.sum(weights[:, None, :] * columns, axis=0)
    live = jnp.arange(obs_dev, dtype=jnp.int32) < obs_count[0]
    result = jnp.where(live[None, :], value, jnp.float32(0.0))
    result = lax.all_gather(result, "member", axis=0, tiled=True)
    return result


def solution(mesh):
    placed = (
        P("member", None, None, "tile"),
        P("member", None, "tile"),
        P(),
        P("tile", None),
        P("tile"),
        P("tile"),
        P("tile"),
        P("tile"),
    )
    return jax.shard_map(
        on_device, mesh=mesh, in_specs=placed, out_specs=P(None, "tile"), check_vma=False
    )
```

profile of v0, /device:TPU:0, one launch (start us, length us, event | category | flops | bytes accessed | tf_op | source)
XLA Modules:
  0.0 90.2 jit_solution(16591186131586178321)
XLA Ops:
  6.5 0.0 copy-start
  6.5 0.7 fusion.3
  7.3 1.1 %reduce-window.6 = s32[16,4,128]{2,0,1:T(8,128)S(1)} reduce-window(s32[16,4,128]{2,0,1:T(8,128)S(1)} %fusion.3, s32[]{:T(128)} %constant.44.clone.1), window={size=1x1x128 pad=0_0x0_0x127_0}, to_apply=%region_0.0 | reduce-window | flops 1040384 | bytes 65540 | tf_op jit(solution)/shard_map/reduce-window
  8.4 0.2 slice_reduce_fusion
  8.7 0.8 fusion.2
  9.4 0.7 and_reduce_fusion
  10.1 2.6 %scatter_custom_fusion = s32[1024]{0:T(1024)S(1)} fusion(s32[512]{0:T(512)S(1)} %bitcast.47, s32[512]{0:T(512)} %param.12, s32[]{:T(128)} %constant.44.clone.1), kind=kCustom, calls=%fused_computation.28 | custom fusion | bytes 4608 | tf_op jit(solution)/shard_map/scatter | solution.py:8
  12.8 0.7 all_to_all.9
  13.4 8.3 %all-to-all-start = ((s32[16,1,64]{2,1,0:T(1,128)}), s32[16,1,64]{2,1,0:T(1,128)S(1)}, u32[]{:S(2)}, u32[]{:S(2)}) async-start(s32[16,1,64]{2,1,0:T(1,128)} %all_to_all.9), calls=%async_computation | async-start | bytes 16384 | tf_op jit(solution)/shard_map/all_to_all | solution.py:26
  21.8 0.0 reduce-scatter.2.cloned.1.call-start
  21.8 0.0 copy-done
  21.8 0.9 convolution_bitcast_fusion
  22.7 1.5 %multiply_reduce_fusion = f32[7,32,128]{2,1,0:T(8,128)S(1)} fusion(bf16[20,7,32,128]{3,2,1,0:T(8,128)(2,1)} %param.8, f32[20,32,128]{2,1,0:T(8,128)S(1)} %convolution_bitcast_fusion), kind=kLoop, calls=%fused_computation.3 | loop fusion | flops 1691648 | bytes 1589248 | tf_op jit(solution)/shard_map/reduce_sum | solution.py:16
  24.2 0.7 copy.17
  24.9 0.0 reduce-scatter.2.cloned.1.call-update
  25.6 3.4 %all-to-all-done = s32[16,1,64]{2,1,0:T(1,128)S(1)} async-done(((s32[16,1,64]{2,1,0:T(1,128)}), s32[16,1,64]{2,1,0:T(1,128)S(1)}, u32[]{:S(2)}, u32[]{:S(2)}) %all-to-all-start) | async-done | bytes 4128 | tf_op jit(solution)/shard_map/all_to_all | solution.py:26
  29.0 0.5 broadcast.138
  29.5 0.7 reduce.7
  30.2 0.1 reshape.144
  30.3 3.7 %reduce-scatter.2.cloned.1.call-done = f32[7,16,128]{2,0,1:T(8,128)} async-done(((f32[7,32,128]{2,0,1:T(8,128)}), f32[7,16,128]{2,0,1:T(8,128)}) %reduce-scatter.2.cloned.1.call-update) | async-done | bytes 57360 | tf_op jit(solution)/shard_map/reduce_scatter | solution.py:17
  34.0 1.1 %copy.18 = f32[7,16,128]{1,0,2:T(8,128)S(1)} copy(f32[7,16,128]{2,0,1:T(8,128)} %reduce-scatter.2.cloned.1.call-done) | data formatting | bytes 114688 | tf_op jit(solution)/shard_map/reduce_scatter | solution.py:17
  35.1 9.1 %gather_fusion = f32[1024,7,16]{2,1,0:T(8,128)} fusion(f32[7,16,128]{1,0,2:T(8,128)S(1)} %copy.18, s32[1024]{0:T(1024)S(1)} %broadcast_clamp_fusion), kind=kCustom, calls=%fused_computation | custom fusion | bytes 921600 | tf_op jit(solution)/shard_map/jit(_take)/gather | solution.py:27
  44.2 2.7 %copy.19 = f32[7,16,16,64]{3,1,0,2:T(8,128)S(1)} copy(f32[7,16,16,64]{1,0,3,2:T(8,128)} %bitcast.40) | data formatting | bytes 917504 | tf_op jit(solution)/shard_map/jit(_take)/gather | solution.py:27
  46.9 0.0 copy-start.2
  46.9 0.0 copy-start.1
  46.9 0.1 fusion.7
  47.0 1.3 %reshape.184 = f32[16,1,7168]{2,1,0:T(1,128)} reshape(f32[16,7,16,64]{3,2,1,0:T(8,128)S(1)} %fusion.7) | data formatting | bytes 917504
  48.3 6.7 %all-to-all-start.1 = ((f32[16,1,7168]{2,1,0:T(1,128)}), f32[16,1,7168]{2,1,0:T(1,128)S(1)}, u32[]{:S(2)}, u32[]{:S(2)}) async-start(f32[16,1,7168]{2,1,0:T(1,128)} %reshape.184), calls=%async_computation.2 | async-start | bytes 917504 | tf_op jit(solution)/shard_map/all_to_all | solution.py:30
  55.1 0.0 copy-done.2
  55.1 0.0 copy-done.1
  55.1 0.3 select_add_fusion
  55.5 13.9 %all-to-all-done.1 = f32[16,1,7168]{2,1,0:T(1,128)S(1)} async-done(((f32[16,1,7168]{2,1,0:T(1,128)}), f32[16,1,7168]{2,1,0:T(1,128)S(1)}, u32[]{:S(2)}, u32[]{:S(2)}) %all-to-all-start.1) | async-done | bytes 458784 | tf_op jit(solution)/shard_map/all_to_all | solution.py:30
  69.4 0.5 broadcast.141
  69.9 1.7 %reduce.8 = f32[16,7168]{1,0:T(8,128)S(1)} reduce(f32[16,1,7168]{2,1,0:T(1,128)S(1)} %all-to-all-done.1, f32[]{:T(128)} %broadcast.141), dimensions={1}, to_apply=%all_to_all.11.reduce_sub_computation | reduce | bytes 917508 | tf_op jit(solution)/shard_map/all_to_all | solution.py:30
  71.7 0.2 reshape.185
  71.9 2.6 %copy.20 = f32[7,16,16,64]{1,0,3,2:T(8,128)} copy(f32[7,16,16,64]{3,1,0,2:T(8,128)S(1)} %bitcast.42) | data formatting | bytes 917504 | tf_op jit(solution)/shard_map/all_to_all | solution.py:30
  74.6 3.2 %gather_fusion.1 = f32[512,7,16]{2,1,0:T(8,128)S(1)} fusion(f32[7,16,1024]{1,0,2:T(8,128)} %bitcast.41, s32[1024]{0:T(1024)S(1)} %pad_clamp_fusion), kind=kCustom, calls=%fused_computation.1 | custom fusion | bytes 460800 | tf_op jit(solution)/shard_map/jit(_take)/gather | solution.py:33
  77.7 2.9 %fusion = f32[16,512]{0,1:T(8,128)S(1)} fusion(f32[512,7,16]{2,1,0:T(8,128)S(1)} %gather_fusion.1, f32[7,512]{0,1:T(8,128)S(1)} %select_add_fusion, pred[512]{0:T(512)(128)(4,1)S(1)} %get-tuple-element.5), kind=kLoop, calls=%fused_computation.5 | loop fusion | flops 163840 | bytes 276992 | tf_op jit(solution)/shard_map/reduce_sum | solution.py:38
  80.7 0.1 broadcast_select_fusion.1
  80.8 0.1 copy.21
  80.9 1.9 %all_gather.3 = f32[32,512]{1,0:T(8,128)S(1)} all-gather(f32[16,512]{1,0:T(8,128)S(1)} %copy.21), channel_id=1, replica_groups=mesh['member'=2,'tile'=16] {'member'}, dimensions={0}, use_global_device_ids=true | all-gather | bytes 98304 | tf_op jit(solution)/shard_map/all_gather | solution.py:41
  82.8 0.6 copy.26
  (9 shorter events, 0.1 us)
Async XLA Ops:
  6.5 15.3 %copy-start = (bf16[20,32,128]{2,1,0:T(8,128)(2,1)S(1)}, bf16[20,32,128]{2,1,0:T(8,128)(2,1)}, u32[]{:S(2)}) copy-start(bf16[20,32,128]{2,1,0:T(8,128)(2,1)} %param.9) | copy-start | bytes 491524
  13.4 15.6 %all-to-all-start = ((s32[16,1,64]{2,1,0:T(1,128)}), s32[16,1,64]{2,1,0:T(1,128)S(1)}, u32[]{:S(2)}, u32[]{:S(2)}) async-start(s32[16,1,64]{2,1,0:T(1,128)} %all_to_all.9), calls=%async_computation | async-start | bytes 16384 | tf_op jit(solution)/shard_map/all_to_all | solution.py:26
  21.8 12.2 %reduce-scatter.2.cloned.1.call-start = ((), (), s32[]{:S(2)}) async-start(), calls=%async_computation.3 | async-start | bytes 196608 | tf_op jit(solution)/shard_map/reduce_scatter | solution.py:17
  46.9 8.2 %copy-start.2 = (s32[512]{0:T(512)S(1)}, s32[512]{0:T(512)}, u32[]{:S(2)}) copy-start(s32[512]{0:T(512)} %param.13) | copy-start | bytes 6148
  46.9 8.2 %copy-start.1 = (f32[512]{0:T(512)S(1)}, f32[512]{0:T(512)}, u32[]{:S(2)}) copy-start(f32[512]{0:T(512)} %param.14) | copy-start | bytes 6148
  48.3 21.1 %all-to-all-start.1 = ((f32[16,1,7168]{2,1,0:T(1,128)}), f32[16,1,7168]{2,1,0:T(1,128)S(1)}, u32[]{:S(2)}, u32[]{:S(2)}) async-start(f32[16,1,7168]{2,1,0:T(1,128)} %reshape.184), calls=%async_computation.2 | async-start | bytes 917504 | tf_op jit(solution)/shard_map/all_to_all | solution.py:30
Sparse Core Ops, SparseCore 0:
  25.1 8.8 reduce-scatter.1
where the time goes:
time: 90.8 us; the launch traced here: 90.2 us
  local copies, waits for them, and re-layouts  26.3 us (29%)
  waiting for transfers between devices  21 us (23%)
  starting transfers between devices  15.1 us (17%)
  between operations  14.2 us (16%)
  other arithmetic  10.8 us (12%)
  blocking collectives  1.85 us (2%)
    all_to_all x1, waiting for transfers between devices, on_device(): lax.all_to_all(picks, 'tile', split_axis=2, concat_axis=2, tiled=True)  13.9 us
    gather x2, local copies, waits for them, and re-layouts, on_device(): jnp.take(increment, got_cols.reshape(-1), axis=2)  11.8 us
    all_to_all x1, starting transfers between devices, on_device(): lax.all_to_all(col_buf, 'tile', split_axis=0, concat_axis=0, tiled=True)  8.34 us
    all_to_all x1, starting transfers between devices, on_device(): lax.all_to_all(picks, 'tile', split_axis=2, concat_axis=2, tiled=True)  6.73 us
    reduce_scatter x1, waiting for transfers between devices, on_device(): lax.psum_scatter(partial_value, 'member', scatter_dimension=1, tiled=True)  3.68 us
    all_to_all x1, waiting for transfers between devices, on_device(): lax.all_to_all(col_buf, 'tile', split_axis=0, concat_axis=0, tiled=True)  3.4 us
    gather x1, local copies, waits for them, and re-layouts, on_device(): columns = jnp.take(returned, flat, axis=2)  3.16 us
    all_to_all x2, local copies, waits for them, and re-layouts, on_device(): lax.all_to_all(picks, 'tile', split_axis=2, concat_axis=2, tiled=True)  3.16 us
  transfers between devices with their start and end apart: 3, of which 3 were waited for; matrix products, arithmetic and copies ran while one was open for 5% of the time, Pallas kernels for 0%

commit v1 on v0

v1 whole, which is shorter than its diff:
```python
import functools

import jax
import jax.numpy as jnp
from jax import lax
from jax.experimental import pallas as pl
from jax.experimental.pallas import tpu as pltpu
from jax.sharding import PartitionSpec as P

MESH = pl.DeviceIdType.MESH
LANES = 128
F32 = jnp.float32
BF16 = jnp.bfloat16


def iota(shape, axis):
    return lax.broadcasted_iota(jnp.int32, shape, axis)


def one_hot(condition):
    return jnp.where(condition, F32(1.0), F32(0.0)).astype(BF16)


def dot(a, b):
    return jnp.dot(a, b, preferred_element_type=F32)


def dot_nt(a, b):
    return lax.dot_general(a, b, (((1,), (1,)), ((), ())), preferred_element_type=F32)


def two_pieces(x):
    high = x.astype(BF16)
    return high, (x - high.astype(F32)).astype(BF16)


def turned(x, shift):
    shift = shift % LANES
    return x if shift == 0 else pltpu.roll(x, shift, 1)


def kernel(
    tiles, groups, cap, packs,
    ens_hbm, ctl_hbm, vloc_ref, source_ref, column_ref, slot_ref, frac_ref, count_ref,
    out_ref,
    ens, ctl, weighted, part, part_in, req_out, req_in, res_out, res_in, place,
    load_sem, part_send, part_recv, req_send, req_recv, res_send, res_recv,
):
    me = lax.axis_index("tile")
    mine = lax.axis_index("member")
    members, slots, levels, cols = ens.shape
    share = levels // groups
    rows = share // packs
    obs = column_ref.shape[1]
    owners = LANES // cap
    spans = tiles * cap // LANES

    def peer(step):
        return lax.rem(me + step, tiles)

    def partner(step):
        return lax.rem(mine + step, groups)

    load_ctl = pltpu.make_async_copy(ctl_hbm, ctl, load_sem.at[0])
    load_ens = pltpu.make_async_copy(ens_hbm, ens, load_sem.at[1])
    load_ctl.start()
    load_ens.start()

    barrier = pltpu.get_barrier_semaphore()

    def greet(index, carry):
        step, side = index // groups, lax.rem(index, groups)
        pl.semaphore_signal(
            barrier, inc=1, device_id={"tile": peer(step), "member": partner(side)},
            device_id_type=MESH,
        )
        return carry

    lax.fori_loop(1, tiles * groups, greet, 0)

    source = source_ref[...]
    hits = source == iota((tiles, obs), 0)
    hits_f = jnp.where(hits, F32(1.0), F32(0.0))
    before = one_hot(iota((LANES, LANES), 0) < iota((LANES, LANES), 1))
    seen = jnp.zeros((tiles, 1), F32)
    ranks = []
    for block in range(obs // LANES):
        hit = hits_f[:, block * LANES:(block + 1) * LANES]
        ahead = dot(hit.astype(BF16), before) + seen
        ranks.append(jnp.sum(ahead * hit, axis=0, keepdims=True))
        seen = seen + jnp.sum(hit, axis=1, keepdims=True)
    rank = jnp.concatenate(ranks, axis=1).astype(jnp.int32)
    spread = one_hot(rank == lax.rem(iota((LANES, obs), 0), cap))
    frac = frac_ref[...]
    frac_0 = frac.astype(BF16).astype(F32)
    frac_1 = (frac - frac_0).astype(BF16).astype(F32)
    frac_2 = frac - frac_0 - frac_1
    values = [column_ref[...].astype(F32), slot_ref[...].astype(F32), frac_0, frac_1, frac_2]
    packed = dot_nt(
        jnp.concatenate([jnp.where(hits, v, F32(0.0)) for v in values], axis=0).astype(BF16), spread
    )
    packed = [packed[i * tiles:(i + 1) * tiles] for i in range(len(values))]
    request = jnp.where(
        iota((tiles, LANES), 1) < cap,
        packed[0] + cols * packed[1],
        packed[2] + packed[3] + packed[4],
    )
    for tile in range(tiles):
        req_out[tile] = request[tile:tile + 1]

    pl.semaphore_wait(barrier, tiles * groups - 1)

    def ask(step):
        return pltpu.make_async_remote_copy(
            src_ref=req_out.at[peer(step)], dst_ref=req_in.at[me],
            send_sem=req_send.at[peer(step)], recv_sem=req_recv.at[me],
            device_id={"tile": peer(step), "member": mine}, device_id_type=MESH,
        )

    def asked(step):
        return pltpu.make_async_remote_copy(
            src_ref=req_out.at[peer(step)], dst_ref=req_in.at[peer(step)],
            send_sem=req_send.at[peer(step)], recv_sem=req_recv.at[peer(step)],
            device_id={"tile": peer(step), "member": mine}, device_id_type=MESH,
        )

    def send_request(step, carry):
        ask(step).start()
        return carry

    lax.fori_loop(1, tiles, send_request, 0)
    req_in[me] = req_out[me]

    batch = max(d for d in range(1, max(1, LANES // levels) + 1) if members % d == 0)
    wide = batch * levels
    repeat = one_hot(lax.rem(iota((wide, levels), 0), levels) == iota((wide, levels), 1))
    tall = dot(repeat, vloc_ref[...]).astype(BF16)
    full = dot_nt(tall, repeat)
    factor = jnp.where(
        iota((wide, wide), 0) // levels == iota((wide, wide), 1) // levels, full, F32(0.0)
    ).astype(BF16)
    load_ctl.wait()
    for step in range(members // batch):
        weighted[step * wide:(step + 1) * wide] = dot(factor, ctl[step * wide:(step + 1) * wide])

    load_ens.wait()
    for slot in range(slots):
        total = jnp.zeros((levels, cols), F32)
        for k in range(members):
            total = total + ens[k, slot].astype(F32) * weighted[k * levels:(k + 1) * levels]
        for group in range(groups):
            part[group, slot] = total[group * share:(group + 1) * share]

    def give(step):
        return pltpu.make_async_remote_copy(
            src_ref=part.at[partner(step)], dst_ref=part_in.at[step - 1],
            send_sem=part_send.at[step - 1], recv_sem=part_recv.at[step - 1],
            device_id={"tile": me, "member": partner(step)}, device_id_type=MESH,
        )

    for step in range(1, groups):
        give(step).start()

    position = source * cap + rank
    place[...] = one_hot(position == iota((tiles * cap, obs), 0))

    for step in range(1, groups):
        give(step).wait_recv()
    increment = part[mine]
    for step in range(1, groups):
        increment = increment + part_in[step - 1]
    pieces = jnp.concatenate(two_pieces(increment.reshape(slots * share, cols)), axis=1)

    def wait_request(step, carry):
        asked(step).wait_recv()
        return carry

    lax.fori_loop(1, tiles, wait_request, 0)

    lane = iota((1, LANES), 1)
    codes, fracs = [], []
    for span in range(spans):
        code = jnp.zeros((1, LANES), F32)
        part_of = jnp.zeros((1, LANES), F32)
        for i in range(owners):
            got = req_in[span * owners + i]
            here = lane // cap == i
            code = jnp.where(here, turned(got, i * cap), code)
            part_of = jnp.where(here, turned(got, i * cap - cap), part_of)
        codes.append(code)
        fracs.append(part_of)
    code = jnp.concatenate(codes, axis=1).astype(jnp.int32)
    frac = jnp.concatenate(fracs, axis=1)
    wanted = code // cols
    column = code - wanted * cols
    width = tiles * cap
    picked = one_hot(lax.rem(iota((2 * cols, width), 0), cols) == column)
    columns = dot(pieces, picked)
    answer = jnp.zeros((share, width), F32)
    for slot in range(slots):
        weight = jnp.where(wanted == slot, 1.0 - frac, jnp.where(wanted + 1 == slot, frac, F32(0.0)))
        answer = answer + weight * columns[slot * share:(slot + 1) * share]
    for owner in range(tiles):
        first = owner * cap // LANES * LANES
        offset = owner * cap % LANES
        packet = jnp.zeros((rows, LANES), F32)
        for j in range(packs):
            block = answer[j * rows:(j + 1) * rows, first:first + LANES]
            packet = jnp.where(lane // cap == j, turned(block, j * cap - offset), packet)
        res_out[owner] = packet

    def reply(index):
        step, side = index // groups, lax.rem(index, groups)
        return pltpu.make_async_remote_copy(
            src_ref=res_out.at[peer(step)], dst_ref=res_in.at[mine, me],
            send_sem=res_send.at[partner(side), peer(step)], recv_sem=res_recv.at[mine, me],
            device_id={"tile": peer(step), "member": partner(side)}, device_id_type=MESH,
        )

    def replied(index):
        step, side = index // groups, lax.rem(index, groups)
        return pltpu.make_async_remote_copy(
            src_ref=res_out.at[peer(step)], dst_ref=res_in.at[partner(side), peer(step)],
            send_sem=res_send.at[partner(side), peer(step)],
            recv_sem=res_recv.at[partner(side), peer(step)],
            device_id={"tile": peer(step), "member": partner(side)}, device_id_type=MESH,
        )

    def send_reply(index, carry):
        reply(index).start()
        return carry

    def wait_reply(index, carry):
        replied(index).wait_recv()
        return carry

    lax.fori_loop(1, tiles * groups, send_reply, 0)
    res_in[mine, me] = res_out[me]
    lax.fori_loop(1, tiles * groups, wait_reply, 0)

    bands = []
    for group in range(groups):
        for j in range(packs):
            band = []
            for span in range(spans):
                tile = jnp.zeros((rows, LANES), F32)
                for i in range(owners):
                    got = res_in[group, span * owners + i]
                    tile = jnp.where(lane // cap == i, turned(got, i * cap - j * cap), tile)
                band.append(tile)
            bands.append(jnp.concatenate(band, axis=1))
    high, low = two_pieces(jnp.concatenate(bands, axis=0))
    both = dot(jnp.concatenate([high, low], axis=0), place[...])
    value = both[:levels] + both[levels:]
    live = iota((levels, obs), 1) < count_ref[0]
    out_ref[...] = jnp.where(live, value, F32(0.0))

    for step in range(1, groups):
        give(step).wait_send()

    def wait_sends(step, carry):
        ask(step).wait_send()
        return carry

    def wait_reply_sends(index, carry):
        reply(index).wait_send()
        return carry

    lax.fori_loop(1, tiles, wait_sends, 0)
    lax.fori_loop(1, tiles * groups, wait_reply_sends, 0)


def on_device(ensemble, control, vert_loc, obs_source, obs_column, obs_slot, obs_frac, obs_count):
    tiles, groups = lax.axis_size("tile"), lax.axis_size("member")
    members, slots, levels, cols = ensemble.shape
    obs = obs_column.shape[0]
    cap = max(4, 2 * obs // tiles)
    share = levels // groups
    packs = max(1, min(LANES // cap, share // 8))
    rows = share // packs
    vmem = pl.BlockSpec(memory_space=pltpu.VMEM)
    hbm = pl.BlockSpec(memory_space=pl.ANY)
    smem = pl.BlockSpec(memory_space=pltpu.SMEM)
    dma = pltpu.SemaphoreType.DMA
    return pl.pallas_call(
        functools.partial(kernel, tiles, groups, cap, packs),
        out_shape=jax.ShapeDtypeStruct((levels, obs), F32),
        in_specs=[hbm, hbm, vmem, vmem, vmem, vmem, vmem, smem],
        out_specs=vmem,
        scratch_shapes=[
            pltpu.VMEM((members, slots, levels, cols), BF16),
            pltpu.VMEM((members * levels, cols), BF16),
            pltpu.VMEM((members * levels, cols), F32),
            pltpu.VMEM((groups, slots, share, cols), F32),
            pltpu.VMEM((max(1, groups - 1), slots, share, cols), F32),
            pltpu.VMEM((tiles, 1, LANES), F32),
            pltpu.VMEM((tiles, 1, LANES), F32),
            pltpu.VMEM((tiles, rows, LANES), F32),
            pltpu.VMEM((groups, tiles, rows, LANES), F32),
            pltpu.VMEM((tiles * cap, obs), BF16),
            dma((2,)),
            dma((max(1, groups - 1),)),
            dma((max(1, groups - 1),)),
            dma((tiles,)),
            dma((tiles,)),
            dma((groups, tiles)),
            dma((groups, tiles)),
        ],
        compiler_params=pltpu.CompilerParams(collective_id=0, has_side_effects=True),
    )(
        ensemble,
        control.reshape(members * levels, cols),
        vert_loc,
        obs_source.reshape(1, obs),
        obs_column.reshape(1, obs),
        obs_slot.reshape(1, obs),
        obs_frac.reshape(1, obs),
        obs_count,
    )


def solution(mesh):
    placed = (
        P("member", None, None, "tile"),
        P("member", None, "tile"),
        P(),
        P("tile", None),
        P("tile"),
        P("tile"),
        P("tile"),
        P("tile"),
    )
    return jax.shard_map(
        on_device, mesh=mesh, in_specs=placed, out_specs=P(None, "tile"), check_vma=False
    )
```

time: 90.8 us -> 21.8 us (0.24)
  local copies, waits for them, and re-layouts: 26.3 us -> 1.47 us
  waiting for transfers between devices: 21 us -> 0 us
  Pallas kernels: 0 us -> 19.5 us
  starting transfers between devices: 15.1 us -> 0 us
  between operations: 14.2 us -> 0.66 us
  other arithmetic: 10.8 us -> 0 us
  blocking collectives: 1.85 us -> 0 us
    pallas_call x0 -> x1, Pallas kernels: none -> 19.5 us  [on_device(): pl.pallas_call(functools.partial(kernel, tiles, groups, cap, packs), out_...]
    all_to_all x2 -> x0, waiting for transfers between devices: 17.3 us -> none  [the longest x1 13.9 us: on_device(): lax.all_to_all(picks, 'tile', split_axis=2, concat_axis=2, tiled=True)]
    all_to_all x2 -> x0, starting transfers between devices: 15.1 us -> none  [the longest x1 8.34 us: on_device(): lax.all_to_all(col_buf, 'tile', split_axis=0, concat_axis=0, tiled=True)]
    gather x3 -> x0, local copies, waits for them, and re-layouts: 15 us -> none  [the longest x2 11.8 us: on_device(): jnp.take(increment, got_cols.reshape(-1), axis=2)]
    reduce_sum x3 -> x0, other arithmetic: 5.23 us -> none  [the longest x1 2.94 us: on_device(): value = jnp.sum(weights[:, None, :] * columns, axis=0)]
    all_to_all x4 -> x0, local copies, waits for them, and re-layouts: 4.34 us -> none  [the longest x2 3.16 us: on_device(): lax.all_to_all(picks, 'tile', split_axis=2, concat_axis=2, tiled=True)]
    reduce_scatter x1 -> x0, waiting for transfers between devices: 3.68 us -> none  [on_device(): lax.psum_scatter(partial_value, 'member', scatter_dimension=1, tiled=True)]
    scatter x1 -> x0, local copies, waits for them, and re-layouts: 2.6 us -> none  [bucket(): return jnp.zeros((length,), values.dtype).at[where_to].set(values)]
  transfers between devices with their start and end apart: 3 -> 0, of which waited for: 3 -> 0; matrix products, arithmetic and copies ran while one was open for 5% -> 0% of each run, Pallas kernels for 0% -> 0%
where the time goes in v1:
time: 21.8 us; the launch traced here: 21.6 us
  Pallas kernels  19.5 us (89%)
  local copies, waits for them, and re-layouts  1.47 us (7%)
  between operations  0.66 us (3%)
    pallas_call x1, Pallas kernels, on_device(): pl.pallas_call(functools.partial(kernel, tiles, groups, cap, packs), out_...  19.5 us
    unnamed x1, local copies, waits for them, and re-layouts  1.47 us

profile of v1, /device:TPU:0, one launch (start us, length us, event | category | flops | bytes accessed | tf_op | source)
XLA Modules:
  0.0 21.6 jit_solution(9859350920856036628)
XLA Ops:
  0.7 19.5 %shard_map.82 = f32[32,512]{1,0:T(8,128)} custom-call(bf16[20,7,32,128]{3,2,1,0:T(8,128)(2,1)} %ens_hbm.1, bf16[640,128]{1,0:T(8,128)(2,1)} %bitcast.5, bf16[32,32]{1,0:T(8,128)(2,1)} %vloc_ref.1, s32[1,512]{1,0:T(1,128)} %bitcast.6, s32[1,512]{1,0:T(1,128)} %bitcast.7, s32[1,512]{1,0:T(1,128)} %bitcast.8, f32[1,512]{1,0:T(1,128)} %bitcast.9, ...), custom_call_target="tpu_custom_call" | custom-call | tf_op jit(solution)/shard_map/pallas_call | solution.py:285
  20.2 1.5 %copy.11 = f32[32,512]{1,0:T(8,128)} copy(f32[32,512]{1,0:T(8,128)} %shard_map.82) | data formatting | bytes 131072

commit v2 on v1

v2 whole, which is shorter than its diff:
```python
import functools

import jax
import jax.numpy as jnp
from jax import lax
from jax.experimental import pallas as pl
from jax.experimental.pallas import tpu as pltpu
from jax.sharding import PartitionSpec as P

MESH = pl.DeviceIdType.MESH
LANES = 128
F32 = jnp.float32
BF16 = jnp.bfloat16


def iota(shape, axis):
    return lax.broadcasted_iota(jnp.int32, shape, axis)


def one_hot(condition):
    return jnp.where(condition, F32(1.0), F32(0.0)).astype(BF16)


def dot(a, b):
    return jnp.dot(a, b, preferred_element_type=F32)


def dot_nt(a, b):
    return lax.dot_general(a, b, (((1,), (1,)), ((), ())), preferred_element_type=F32)


def two_pieces(x):
    high = x.astype(BF16)
    return high, (x - high.astype(F32)).astype(BF16)


def turned(x, shift):
    shift = shift % LANES
    return x if shift == 0 else pltpu.roll(x, shift, 1)


def kernel(
    tiles, groups, cap, packs,
    ens_hbm, ctl_hbm, vloc_hbm, source_hbm, column_hbm, slot_hbm, frac_hbm, count_ref,
    out_ref,
    vloc_ref, source_ref, column_ref, slot_ref, frac_ref, ens, ctl, weighted, part, part_in, req_out, req_in, res_out, res_in, place,
    load_sem, part_send, part_recv, req_send, req_recv, res_send, res_recv,
):
    me = lax.axis_index("tile")
    mine = lax.axis_index("member")
    members, slots, levels, cols = ens.shape
    share = levels // groups
    rows = share // packs
    obs = column_ref.shape[1]
    owners = LANES // cap
    spans = tiles * cap // LANES

    def loaded(index, source, target):
        return pltpu.make_async_copy(source, target, load_sem.at[index])

    loads = [
        loaded(0, source_hbm, source_ref), loaded(1, column_hbm, column_ref),
        loaded(2, slot_hbm, slot_ref), loaded(3, frac_hbm, frac_ref),
        loaded(4, vloc_hbm, vloc_ref), loaded(5, ctl_hbm, ctl), loaded(6, ens_hbm, ens),
    ]
    for load in loads[:4]:
        load.start()

    stride = jnp.where(2 * me < tiles, 1, tiles - 1)
    span_stride = jnp.where(2 * me < tiles, 1, spans - 1)
    home = me // owners

    def peer(step):
        return lax.rem(me + stride * step, tiles)

    def span_at(step):
        return lax.rem(home + span_stride * step, spans)

    def partner(step):
        return lax.rem(mine + step, groups)

    def far_first(count, body):
        if count <= 64:
            for index in range(count - 1, 0, -1):
                body(index)
        else:
            lax.fori_loop(1, count, lambda index, carry: (body(index), carry)[1], 0)

    barrier = pltpu.get_barrier_semaphore()

    def greet(index):
        step, side = index // groups, index % groups
        pl.semaphore_signal(
            barrier, inc=1, device_id={"tile": peer(step), "member": partner(side)},
            device_id_type=MESH,
        )

    far_first(tiles * groups, greet)
    for load in loads[4:]:
        load.start()

    for load in loads[:4]:
        load.wait()
    source = source_ref[...]
    hits = source == iota((tiles, obs), 0)
    hits_f = jnp.where(hits, F32(1.0), F32(0.0))
    before = one_hot(iota((LANES, LANES), 0) < iota((LANES, LANES), 1))
    seen = jnp.zeros((tiles, 1), F32)
    ranks = []
    for block in range(obs // LANES):
        hit = hits_f[:, block * LANES:(block + 1) * LANES]
        ahead = dot(hit.astype(BF16), before) + seen
        ranks.append(jnp.sum(ahead * hit, axis=0, keepdims=True))
        seen = seen + jnp.sum(hit, axis=1, keepdims=True)
    rank = jnp.concatenate(ranks, axis=1).astype(jnp.int32)
    spread = one_hot(rank == lax.rem(iota((LANES, obs), 0), cap))
    frac = frac_ref[...]
    frac_0 = frac.astype(BF16).astype(F32)
    frac_1 = (frac - frac_0).astype(BF16).astype(F32)
    frac_2 = frac - frac_0 - frac_1
    values = [column_ref[...].astype(F32), slot_ref[...].astype(F32), frac_0, frac_1, frac_2]
    packed = dot_nt(
        jnp.concatenate([jnp.where(hits, v, F32(0.0)) for v in values], axis=0).astype(BF16), spread
    )
    packed = [packed[i * tiles:(i + 1) * tiles] for i in range(len(values))]
    request = jnp.where(
        iota((tiles, LANES), 1) < cap,
        packed[0] + cols * packed[1],
        packed[2] + packed[3] + packed[4],
    )
    for tile in range(tiles):
        req_out[tile] = request[tile:tile + 1]

    pl.semaphore_wait(barrier, tiles * groups - 1)

    def request_to(tile, slot_of):
        return pltpu.make_async_remote_copy(
            src_ref=req_out.at[tile], dst_ref=req_in.at[slot_of],
            send_sem=req_send.at[tile], recv_sem=req_recv.at[slot_of],
            device_id={"tile": tile, "member": mine}, device_id_type=MESH,
        )

    far_first(tiles, lambda step: request_to(peer(step), me).start())
    req_in[me] = req_out[me]

    batch = max(d for d in range(1, max(1, LANES // levels) + 1) if members % d == 0)
    wide = batch * levels
    repeat = one_hot(lax.rem(iota((wide, levels), 0), levels) == iota((wide, levels), 1))
    for load in loads[4:6]:
        load.wait()
    tall = dot(repeat, vloc_ref[...]).astype(BF16)
    full = dot_nt(tall, repeat)
    factor = jnp.where(
        iota((wide, wide), 0) // levels == iota((wide, wide), 1) // levels, full, F32(0.0)
    ).astype(BF16)
    for step in range(members // batch):
        weighted[step * wide:(step + 1) * wide] = dot(factor, ctl[step * wide:(step + 1) * wide])

    loads[6].wait()
    for slot in range(slots):
        total = jnp.zeros((levels, cols), F32)
        for k in range(members):
            total = total + ens[k, slot].astype(F32) * weighted[k * levels:(k + 1) * levels]
        for group in range(groups):
            part[group, slot] = total[group * share:(group + 1) * share]

    def give(step):
        return pltpu.make_async_remote_copy(
            src_ref=part.at[partner(step)], dst_ref=part_in.at[step - 1],
            send_sem=part_send.at[step - 1], recv_sem=part_recv.at[step - 1],
            device_id={"tile": me, "member": partner(step)}, device_id_type=MESH,
        )

    for step in range(1, groups):
        give(step).start()

    position = source * cap + rank
    place[...] = one_hot(position == iota((tiles * cap, obs), 0))

    for step in range(1, groups):
        give(step).wait_recv()
    increment = part[mine]
    for step in range(1, groups):
        increment = increment + part_in[step - 1]
    pieces = jnp.concatenate(two_pieces(increment.reshape(slots * share, cols)), axis=1)

    def reply_to(tile, side, slot_of, from_group):
        return pltpu.make_async_remote_copy(
            src_ref=res_out.at[tile], dst_ref=res_in.at[from_group, slot_of],
            send_sem=res_send.at[partner(side), tile], recv_sem=res_recv.at[from_group, slot_of],
            device_id={"tile": tile, "member": partner(side)}, device_id_type=MESH,
        )

    def unless_me(step, tile, body):
        if step == 0:
            pl.when(tile != me)(body)
        else:
            body()

    lane = iota((1, LANES), 1)
    for step in range(spans):
        span = span_at(step)
        code = jnp.zeros((1, LANES), F32)
        frac = jnp.zeros((1, LANES), F32)
        for i in range(owners):
            tile = span * owners + i
            unless_me(step, tile, lambda tile=tile: request_to(tile, tile).wait_recv())
            got = req_in[tile]
            here = lane // cap == i
            code = jnp.where(here, turned(got, i * cap), code)
            frac = jnp.where(here, turned(got, i * cap - cap), frac)
        code = code.astype(jnp.int32)
        wanted = code // cols
        column = code - wanted * cols
        columns = dot(pieces, one_hot(lax.rem(iota((2 * cols, LANES), 0), cols) == column))
        answer = jnp.zeros((share, LANES), F32)
        for slot in range(slots):
            weight = jnp.where(
                wanted == slot, 1.0 - frac, jnp.where(wanted + 1 == slot, frac, F32(0.0))
            )
            answer = answer + weight * columns[slot * share:(slot + 1) * share]
        for i in range(owners):
            tile = span * owners + i
            packet = jnp.zeros((rows, LANES), F32)
            for j in range(packs):
                block = answer[j * rows:(j + 1) * rows]
                packet = jnp.where(lane // cap == j, turned(block, (j - i) * cap), packet)
            res_out[tile] = packet
            if step == 0:
                @pl.when(tile == me)
                def _():
                    res_in[mine, me] = packet
            for side in range(groups):
                if side == 0:
                    unless_me(step, tile, lambda tile=tile: reply_to(tile, 0, me, mine).start())
                else:
                    reply_to(tile, side, me, mine).start()

    for step in range(1, groups):
        give(step).wait_send()

    def wait_reply_send(index):
        reply_to(peer(index // groups), index % groups, me, mine).wait_send()

    far_first(tiles, lambda step: request_to(peer(step), me).wait_send())
    far_first(tiles * groups, wait_reply_send)

    live = iota((levels, obs), 1) < count_ref[0]
    both = jnp.zeros((2 * levels, obs), F32)
    for step in range(spans):
        span = span_at(step)
        bands = [jnp.zeros((rows, LANES), F32)] * (groups * packs)
        for side in range(groups):
            for i in range(owners):
                tile = span * owners + i
                body = lambda tile=tile, side=side: reply_to(tile, side, tile, partner(side)).wait_recv()
                if side == 0:
                    unless_me(step, tile, body)
                else:
                    body()
        for group in range(groups):
            for i in range(owners):
                got = res_in[group, span * owners + i]
                for j in range(packs):
                    at = group * packs + j
                    bands[at] = jnp.where(lane // cap == i, turned(got, (i - j) * cap), bands[at])
        high, low = two_pieces(jnp.concatenate(bands, axis=0))
        first = pl.multiple_of(span * LANES, LANES)
        both = both + dot(jnp.concatenate([high, low], axis=0), place[pl.ds(first, LANES)])
    out_ref[...] = jnp.where(live, both[:levels] + both[levels:], F32(0.0))


def on_device(ensemble, control, vert_loc, obs_source, obs_column, obs_slot, obs_frac, obs_count):
    tiles, groups = lax.axis_size("tile"), lax.axis_size("member")
    members, slots, levels, cols = ensemble.shape
    obs = obs_column.shape[0]
    cap = max(4, 2 * obs // tiles)
    share = levels // groups
    packs = max(1, min(LANES // cap, share // 8))
    rows = share // packs
    vmem = pl.BlockSpec(memory_space=pltpu.VMEM)
    hbm = pl.BlockSpec(memory_space=pl.ANY)
    dma = pltpu.SemaphoreType.DMA
    return pl.pallas_call(
        functools.partial(kernel, tiles, groups, cap, packs),
        out_shape=pltpu.VMEM((levels, obs), F32),
        in_specs=[hbm] * 7 + [pl.BlockSpec(memory_space=pltpu.SMEM)],
        out_specs=vmem,
        scratch_shapes=[
            pltpu.VMEM((levels, levels), BF16),
            pltpu.VMEM((1, obs), jnp.int32),
            pltpu.VMEM((1, obs), jnp.int32),
            pltpu.VMEM((1, obs), jnp.int32),
            pltpu.VMEM((1, obs), F32),
            pltpu.VMEM((members, slots, levels, cols), BF16),
            pltpu.VMEM((members * levels, cols), BF16),
            pltpu.VMEM((members * levels, cols), F32),
            pltpu.VMEM((groups, slots, share, cols), F32),
            pltpu.VMEM((max(1, groups - 1), slots, share, cols), F32),
            pltpu.VMEM((tiles, 1, LANES), F32),
            pltpu.VMEM((tiles, 1, LANES), F32),
            pltpu.VMEM((tiles, rows, LANES), F32),
            pltpu.VMEM((groups, tiles, rows, LANES), F32),
            pltpu.VMEM((tiles * cap, obs), BF16),
            dma((7,)),
            dma((max(1, groups - 1),)),
            dma((max(1, groups - 1),)),
            dma((tiles,)),
            dma((tiles,)),
            dma((groups, tiles)),
            dma((groups, tiles)),
        ],
        compiler_params=pltpu.CompilerParams(collective_id=0, has_side_effects=True),
    )(
        ensemble,
        control.reshape(members * levels, cols),
        vert_loc,
        obs_source.reshape(1, obs),
        obs_column.reshape(1, obs),
        obs_slot.reshape(1, obs),
        obs_frac.reshape(1, obs),
        obs_count,
    )


def solution(mesh):
    placed = (
        P("member", None, None, "tile"),
        P("member", None, "tile"),
        P(),
        P("tile", None),
        P("tile"),
        P("tile"),
        P("tile"),
        P("tile"),
    )
    return jax.shard_map(
        on_device, mesh=mesh, in_specs=placed, out_specs=P(None, "tile"), check_vma=False
    )
```

time: 21.8 us -> 19.1 us (0.88)
  Pallas kernels: 19.5 us -> 17.6 us
  local copies, waits for them, and re-layouts: 1.47 us -> 0.63 us
    pallas_call x1, Pallas kernels: 19.5 us -> 17.6 us  [on_device(): pl.pallas_call(functools.partial(kernel, tiles, groups, cap, packs), out_...]
    unnamed x1, local copies, waits for them, and re-layouts: 1.47 us -> 0.63 us
where the time goes in v2:
time: 19.1 us; the launch traced here: 18.9 us
  Pallas kernels  17.6 us (92%)
  between operations  0.66 us (3%)
  local copies, waits for them, and re-layouts  0.63 us (3%)
    pallas_call x1, Pallas kernels, on_device(): pl.pallas_call(functools.partial(kernel, tiles, groups, cap, packs), out_...  17.6 us
    unnamed x1, local copies, waits for them, and re-layouts  0.63 us

profile of v2, /device:TPU:0, one launch (start us, length us, event | category | flops | bytes accessed | tf_op | source)
XLA Modules:
  0.0 18.9 jit_solution(16798717817660324605)
XLA Ops:
  0.7 17.6 %shard_map.82 = f32[32,512]{1,0:T(8,128)S(1)} custom-call(bf16[20,7,32,128]{3,2,1,0:T(8,128)(2,1)} %ens_hbm.1, bf16[640,128]{1,0:T(8,128)(2,1)} %bitcast.5, bf16[32,32]{1,0:T(8,128)(2,1)} %vloc_hbm.1, s32[1,512]{1,0:T(1,128)} %bitcast.6, s32[1,512]{1,0:T(1,128)} %bitcast.7, s32[1,512]{1,0:T(1,128)} %bitcast.8, f32[1,512]{1,0:T(1,128)} %bitcast.9, ...), custom_call_target="tpu_custom_call" | custom-call | tf_op jit(solution)/shard_map/pallas_call | solution.py:284
  18.3 0.6 %copy.10 = f32[32,512]{1,0:T(8,128)} copy(f32[32,512]{1,0:T(8,128)S(1)} %shard_map.82) | data formatting | bytes 131072
